TPU v7x, 32 devices: a whole 2x2x4 slice. The times are simulated.
32 devices in a mesh: gz: 8 (over y, x, core), gx: 4 (over z).
Axes of the slice: x: 2, y: 2, z: 4, core: 2. Of those that a mesh axis runs over, the one named last changes fastest.
Arguments:
- density: float32 [512, 128, 128], P('gz', 'gx'), may hold values from -6 to 6
- velocity: float32 [3, 512, 128, 128], P(None, 'gz', 'gx'), may hold values from -6 to 6
- labels: int32 [512, 128, 128], P('gz', 'gx'), may hold values from 0 to 7
- sound_table: float32 [8], replicated, may hold values from 0.8 to 1.6
- mass_table: float32 [8], replicated, may hold values from 0.8 to 2
- source_index: int32 [4096], replicated, may hold values from 0 to 8388607
- source_values: float32 [1, 4096], replicated, may hold values from -6 to 6
Outputs:
- new_density: float32 [512, 128, 128], P('gz', 'gx')
- new_velocity: float32 [3, 512, 128, 128], P(None, 'gz', 'gx')
Inputs may be any that keep to these rules, and one draw needn't show every extreme that they name: `source_index`: flat cell index z * 128 * 128 + x * 128 + y; an index may repeat.
All inputs are finite; a program needn't handle non-finite values.
Results may differ from a plain program's by a relative error of at most 0.00011.
Values sent between devices are 32-bit elements; how exact they have to be, the bound alone decides.
A program may use at most 128 MiB of HBM per device.

v0:
```python
import math

import jax
import jax.numpy as jnp
from jax import lax
from jax.sharding import PartitionSpec as P

NZ = 512
NX = 128
NY = 128
LABELS = 8
PML_W = 20


time_step = 0.3
absorb = 2.0
highest = lax.Precision.HIGHEST


def signed_wave(positions, length):
    signed = jnp.where(positions < length // 2, positions, positions - length)
    return 2.0 * math.pi / length * signed.astype(jnp.float32)


def damping(positions, length, speed_ref):
    coordinate = positions.astype(jnp.float32)
    layer_depth = (
        jnp.maximum(jnp.maximum(PML_W - coordinate, coordinate - (length - 1 - PML_W)), 0.0) / PML_W
    )
    return jnp.exp(-absorb * speed_ref * layer_depth**4 * time_step * 0.5)


def dft_table(length, inverse):
    positions = jnp.arange(length, dtype=jnp.int32)
    phases = (
        2.0
        * math.pi
        / length
        * (positions[:, None] * positions[None, :] % length).astype(jnp.float32)
    )
    if inverse:
        return (jnp.cos(phases) / length, jnp.sin(phases) / length)
    return (jnp.cos(phases), -jnp.sin(phases))


def twiddle_table(length, inverse):
    first_idx = jnp.arange(4, dtype=jnp.int32)
    second = jnp.arange(length // 4, dtype=jnp.int32)
    phases = (
        2.0 * math.pi / length * (first_idx[:, None] * second[None, :] % length).astype(jnp.float32)
    )
    if inverse:
        return (jnp.cos(phases), jnp.sin(phases))
    return (jnp.cos(phases), -jnp.sin(phases))


def derivative(wave, orient):
    return (-orient * wave * jnp.sin(0.5 * wave), wave * jnp.cos(0.5 * wave))


def contract(formula, operand, matrix):
    return jnp.einsum(
        formula, operand, matrix, precision=highest, preferred_element_type=jnp.float32
    )


def matrix_step(formula, spectra, dft_pair):
    return (
        contract(formula, spectra[0], dft_pair[0]) - contract(formula, spectra[1], dft_pair[1]),
        contract(formula, spectra[0], dft_pair[1]) + contract(formula, spectra[1], dft_pair[0]),
    )


def complex_times(operand, factor):
    return (
        operand[0] * factor[0] - operand[1] * factor[1],
        operand[0] * factor[1] + operand[1] * factor[0],
    )


def take_fields(spectra, first_row, last_row):
    return (spectra[0][first_row:last_row], spectra[1][first_row:last_row])


def long_transform(spectra, tables):
    quarter, twiddle, long_tab = tables
    fields, length, rows_x, cols_k = spectra[0].shape
    divided = tuple(
        (portion.reshape(fields, 4, length // 4, rows_x, cols_k) for portion in spectra)
    )
    blended = matrix_step("bpnxk,pq->bqnxk", divided, quarter)
    turned = complex_times(
        blended, (twiddle[0][None, :, :, None, None], twiddle[1][None, :, :, None, None])
    )
    result = matrix_step("bqnxk,nm->bxkqm", turned, long_tab)
    return tuple((portion.reshape(fields, rows_x, cols_k, length) for portion in result))


def long_inverse_transform(spectra, tables):
    quarter, twiddle, long_tab = tables
    fields, rows_x, cols_k, length = spectra[0].shape
    divided = tuple(
        (portion.reshape(fields, rows_x, cols_k, 4, length // 4) for portion in spectra)
    )
    blended = matrix_step("bxkqm,mn->bqnxk", divided, long_tab)
    turned = complex_times(
        blended, (twiddle[0][None, :, :, None, None], twiddle[1][None, :, :, None, None])
    )
    result = matrix_step("bqnxk,qp->bpnxk", turned, quarter)
    return tuple((portion.reshape(fields, length, rows_x, cols_k) for portion in result))


def lateral_forward(spectra, after_fn):
    return after_fn(
        (
            lax.all_to_all(spectra[0], "gx", split_axis=3, concat_axis=2, tiled=True),
            lax.all_to_all(spectra[1], "gx", split_axis=3, concat_axis=2, tiled=True),
        )
    )


def long_forward(spectra, after_fn):
    return after_fn(
        (
            lax.all_to_all(spectra[0], "gz", split_axis=2, concat_axis=1, tiled=True),
            lax.all_to_all(spectra[1], "gz", split_axis=2, concat_axis=1, tiled=True),
        )
    )


def long_inverse(spectra, after_fn):
    return after_fn(
        (
            lax.all_to_all(spectra[0], "gz", split_axis=1, concat_axis=2, tiled=True),
            lax.all_to_all(spectra[1], "gz", split_axis=1, concat_axis=2, tiled=True),
        )
    )


def lateral_inverse(spectra, after_fn):
    return after_fn(
        (
            lax.all_to_all(spectra[0], "gx", split_axis=2, concat_axis=3, tiled=True),
            lax.all_to_all(spectra[1], "gx", split_axis=2, concat_axis=3, tiled=True),
        )
    )


def add_sources(density, source_index, amounts, z_start, x_start):
    z_local, x_local, y_count = density.shape
    plane_size = NX * NY
    z_offset = source_index // plane_size - z_start
    remain = source_index % plane_size
    x_offset = remain // NY - x_start
    y_offset = remain % NY
    inside = (z_offset >= 0) & (z_offset < z_local) & (x_offset >= 0) & (x_offset < x_local)
    flat_index = jnp.where(
        inside, (z_offset * x_local + x_offset) * y_count + y_offset, z_local * x_local * y_count
    )
    return density.reshape(-1).at[flat_index].add(amounts, mode="drop").reshape(density.shape)


def shards(density, velocity, labels, sound_table, mass_table, source_index, source_values):
    z_local, x_local, y_count = density.shape
    z_start = lax.axis_index("gz") * z_local
    x_start = lax.axis_index("gx") * x_local
    speed_sq = jnp.zeros(density.shape, jnp.float32)
    rho_zero = jnp.zeros(density.shape, jnp.float32)
    for tissue in range(LABELS):
        chosen = labels == tissue
        speed_sq = jnp.where(chosen, sound_table[tissue] ** 2, speed_sq)
        rho_zero = jnp.where(chosen, mass_table[tissue], rho_zero)
    speed_ref = jnp.max(sound_table)
    damp_z = damping(z_start + jnp.arange(z_local, dtype=jnp.int32), NZ, speed_ref)[:, None, None]
    damp_x = damping(x_start + jnp.arange(x_local, dtype=jnp.int32), NX, speed_ref)[None, :, None]
    damp_y = damping(jnp.arange(y_count, dtype=jnp.int32), NY, speed_ref)[None, None, :]
    damp_all = damp_z * damp_x * damp_y
    damp_axes = jnp.stack(
        [jnp.broadcast_to(profile, density.shape) for profile in (damp_z, damp_x, damp_y)]
    )
    kx_local = NX // lax.axis_size("gz")
    ky_local = NY // lax.axis_size("gx")
    wave_x = signed_wave(
        lax.axis_index("gz") * kx_local + jnp.arange(kx_local, dtype=jnp.int32), NX
    )[:, None, None]
    wave_y = signed_wave(
        lax.axis_index("gx") * ky_local + jnp.arange(ky_local, dtype=jnp.int32), NY
    )[None, :, None]
    position = jnp.arange(NZ, dtype=jnp.int32)
    quarter_len = NZ // 4
    wave_z = signed_wave(position // quarter_len + 4 * (position % quarter_len), NZ)[None, None, :]
    correction = jnp.sinc(
        speed_ref * jnp.sqrt(wave_z**2 + wave_x**2 + wave_y**2) * time_step / (2.0 * math.pi)
    )
    y_fwd = dft_table(NY, False)
    y_inv = dft_table(NY, True)
    x_fwd = dft_table(NX, False)
    x_inv = dft_table(NX, True)
    z_fwd = (dft_table(4, False), twiddle_table(NZ, False), dft_table(NZ // 4, False))
    z_inv = (dft_table(4, True), twiddle_table(NZ, True), dft_table(NZ // 4, True))

    def x_forward(spectra):
        return matrix_step("bzxk,xm->bzmk", spectra, x_fwd)

    def x_inverse(spectra):
        return matrix_step("bzmk,mx->bzxk", spectra, x_inv)

    def y_inverse(spectra):
        return contract("bzxk,ky->bzxy", spectra[0], y_inv[0]) - contract(
            "bzxk,ky->bzxy", spectra[1], y_inv[1]
        )

    def z_forward(spectra):
        return long_transform(spectra, z_fwd)

    plus_pairs = [derivative(wave, 1.0) for wave in (wave_z, wave_x, wave_y)]
    minus_pairs = [derivative(wave, -1.0) for wave in (wave_z, wave_x, wave_y)]
    grad_scaled = [
        (correction * factor_pair[0], correction * factor_pair[1]) for factor_pair in plus_pairs
    ]
    div_scaled = [
        (correction * factor_pair[0], correction * factor_pair[1]) for factor_pair in minus_pairs
    ]
    packed_grad = (
        jnp.stack([grad_scaled[0][0] - grad_scaled[1][1], grad_scaled[2][0]]),
        jnp.stack([grad_scaled[0][1] + grad_scaled[1][0], grad_scaled[2][1]]),
    )
    packed_div = (
        jnp.stack([div_scaled[0][0] + div_scaled[1][1], div_scaled[2][0]]),
        jnp.stack([div_scaled[0][1] - div_scaled[1][0], div_scaled[2][1]]),
    )

    def y_split(spectra):
        first = matrix_step("bzxk,ky->bzxy", take_fields(spectra, 0, 1), y_inv)
        return jnp.concatenate([first[0], first[1], y_inverse(take_fields(spectra, 1, 2))])

    pressure = speed_sq * density
    field = pressure[None]
    spectrum = long_forward(
        lateral_forward(
            (
                contract("bzxy,yk->bzxk", field, y_fwd[0]),
                contract("bzxy,yk->bzxk", field, y_fwd[1]),
            ),
            x_forward,
        ),
        z_forward,
    )
    sectioned = long_inverse_transform(complex_times(spectrum, packed_grad), z_inv)
    slopes = lateral_inverse(long_inverse(sectioned, x_inverse), y_split)
    velocity = damp_axes * (damp_axes * velocity - time_step / rho_zero * slopes)
    packed = (
        jnp.stack([velocity[0], velocity[2]]),
        jnp.stack([velocity[1], jnp.zeros_like(velocity[2])]),
    )
    spectra = long_forward(
        lateral_forward(matrix_step("bzxy,yk->bzxk", packed, y_fwd), x_forward), z_forward
    )
    product = complex_times(spectra, packed_div)
    sectioned = long_inverse_transform(
        (jnp.sum(product[0], axis=0, keepdims=True), jnp.sum(product[1], axis=0, keepdims=True)),
        z_inv,
    )
    spread = lateral_inverse(long_inverse(sectioned, x_inverse), y_inverse)[0]
    density = damp_all * (damp_all * density - time_step * rho_zero * spread)
    density = add_sources(density, source_index, source_values[0], z_start, x_start)
    return (density, velocity)


def solution(mesh):
    in_specs = (
        P("gz", "gx", None),
        P(None, "gz", "gx", None),
        P("gz", "gx", None),
        P(),
        P(),
        P(),
        P(),
    )
    out_specs = (P("gz", "gx", None), P(None, "gz", "gx", None))
    return jax.shard_map(shards, mesh=mesh, in_specs=in_specs, out_specs=out_specs, check_vma=False)
```

profile of v0, /device:TPU:9, one launch (start us, length us, event | category | flops | bytes accessed | tf_op | source)
XLA Modules:
  0.0 926.1 jit_solution(6921629593954702259)
XLA Ops:
  13.8 8.4 broadcast_divide_fusion
  41.5 16.4 %all-to-all-done = f32[4,1,65536]{2,1,0:T(1,128)} async-done(((f32[4,1,65536]{2,1,0:T(1,128)}), f32[4,1,65536]{2,1,0:T(1,128)}, u32[]{:S(2)}, u32[]{:S(2)}) %all-to-all-start) | async-done | bytes 1048608 | tf_op jit(solution)/shard_map/all_to_all | solution.py:116
  57.8 8.2 all-to-all-start.1
  79.1 7.9 all-to-all-done.1
  109.7 6.4 all-to-all-start.2
  128.0 8.0 all-to-all-start.3
  198.2 5.8 add_bitcast_fusion.3
  204.0 6.4 copy.398
  210.3 8.6 reshape.764
  223.2 6.5 fusion.27
  235.2 6.4 copy.395
  241.5 8.6 reshape.762
  254.7 7.2 reduce.7
  261.9 6.0 reshape.765
  267.9 7.2 copy.317
  279.1 8.5 reduce.6
  287.7 7.6 reshape.763
  295.3 7.2 copy.311
  326.1 7.5 all-to-all-start.6
  352.0 24.7 %all-to-all-done.6 = f32[4,1,131072]{2,1,0:T(1,128)} async-done(((f32[4,1,131072]{2,1,0:T(1,128)}), f32[4,1,131072]{2,1,0:T(1,128)}, u32[]{:S(2)}, u32[]{:S(2)}) %all-to-all-start.6) | async-done | bytes 2097184 | tf_op jit(solution)/shard_map/all_to_all | solution.py:143
  376.7 9.4 %all-to-all-start.7 = ((f32[4,1,131072]{2,1,0:T(1,128)}), f32[4,1,131072]{2,1,0:T(1,128)}, u32[]{:S(2)}, u32[]{:S(2)}) async-start(f32[4,1,131072]{2,1,0:T(1,128)} %reshape.768), calls=%async_computation.7 | async-start | bytes 4194304 | tf_op jit(solution)/shard_map/all_to_all | solution.py:144
  386.1 7.7 reduce.8
  408.2 21.6 %all-to-all-done.7 = f32[4,1,131072]{2,1,0:T(1,128)} async-done(((f32[4,1,131072]{2,1,0:T(1,128)}), f32[4,1,131072]{2,1,0:T(1,128)}, u32[]{:S(2)}, u32[]{:S(2)}) %all-to-all-start.7) | async-done | bytes 2097184 | tf_op jit(solution)/shard_map/all_to_all | solution.py:144
  429.8 7.7 reduce.9
  471.1 5.6 copy.339
  482.3 8.5 all-to-all-start.9
  505.1 29.6 %all-to-all-done.9 = f32[4,1,131072]{2,1,0:T(1,128)} async-done(((f32[4,1,131072]{2,1,0:T(1,128)}), f32[4,1,131072]{2,1,0:T(1,128)}, u32[]{:S(2)}, u32[]{:S(2)}) %all-to-all-start.9) | async-done | bytes 2097184 | tf_op jit(solution)/shard_map/all_to_all | solution.py:117
  534.7 8.4 all-to-all-start.8
  543.1 7.7 reduce.11
  554.7 6.6 copy.341
  565.5 21.5 %all-to-all-done.8 = f32[4,1,131072]{2,1,0:T(1,128)} async-done(((f32[4,1,131072]{2,1,0:T(1,128)}), f32[4,1,131072]{2,1,0:T(1,128)}, u32[]{:S(2)}, u32[]{:S(2)}) %all-to-all-start.8) | async-done | bytes 2097184 | tf_op jit(solution)/shard_map/all_to_all | solution.py:116
  587.0 9.1 reduce.10
  601.6 6.6 copy.337
  625.9 7.2 reshape.774
  633.1 6.5 all-to-all-start.10
  652.5 7.2 reshape.776
  662.7 8.3 all-to-all-start.11
  671.1 7.2 reduce.12
  681.9 8.0 copy.345
  703.1 7.2 reduce.13
  713.9 8.0 copy.350
  779.3 7.3 all-to-all-start.12
  825.3 7.3 all-to-all-start.15
  839.4 14.4 %all-to-all-done.15 = f32[4,1,65536]{2,1,0:T(1,128)} async-done(((f32[4,1,65536]{2,1,0:T(1,128)}), f32[4,1,65536]{2,1,0:T(1,128)}, u32[]{:S(2)}, u32[]{:S(2)}) %all-to-all-start.15) | async-done | bytes 1048608 | tf_op jit(solution)/shard_map/all_to_all | solution.py:144
  853.8 8.6 all-to-all-start.14
  873.1 10.6 %all-to-all-done.14 = f32[4,1,65536]{2,1,0:T(1,128)} async-done(((f32[4,1,65536]{2,1,0:T(1,128)}), f32[4,1,65536]{2,1,0:T(1,128)}, u32[]{:S(2)}, u32[]{:S(2)}) %all-to-all-start.14) | async-done | bytes 1048608 | tf_op jit(solution)/shard_map/all_to_all | solution.py:143
  895.0 7.1 multiply_multiply_fusion
  902.1 22.8 %scatter_fusion = f32[262144]{0:T(1024)S(1)} fusion(f32[262144]{0:T(1024)S(1)} %bitcast.463, s32[4096]{0:T(1024)S(1)} %compare_select_fusion, f32[4096]{0:T(1024)S(1)} %bitcast.525), kind=kCustom, calls=%fused_computation | custom fusion | flops 4096 | bytes 65536 | tf_op jit(solution)/shard_map/scatter-add | solution.py:160
  (287 shorter events, 452.2 us)
Async XLA Ops:
  13.8 8.5 copy-start.19
  31.2 26.6 %all-to-all-start = ((f32[4,1,65536]{2,1,0:T(1,128)}), f32[4,1,65536]{2,1,0:T(1,128)}, u32[]{:S(2)}, u32[]{:S(2)}) async-start(f32[4,1,65536]{2,1,0:T(1,128)} %reshape.754), calls=%async_computation | async-start | bytes 2097152 | tf_op jit(solution)/shard_map/all_to_all | solution.py:116
  39.1 26.9 %copy-start.45 = (f32[8]{0:T(128)S(1)}, f32[8]{0:T(128)}, u32[]{:S(2)}) copy-start(f32[8]{0:T(128)} %param.10) | copy-start | bytes 100
  57.8 29.2 %all-to-all-start.1 = ((f32[4,1,65536]{2,1,0:T(1,128)}), f32[4,1,65536]{2,1,0:T(1,128)}, u32[]{:S(2)}, u32[]{:S(2)}) async-start(f32[4,1,65536]{2,1,0:T(1,128)} %reshape.756), calls=%async_computation.1 | async-start | bytes 2097152 | tf_op jit(solution)/shard_map/all_to_all | solution.py:117
  67.5 123.8 %copy-start.46 = (f32[4,128]{1,0:T(4,128)}, f32[4,128]{1,0:T(4,128)S(1)}, u32[]{:S(2)}) copy-start(f32[4,128]{1,0:T(4,128)S(1)} %fusion.235) | copy-start | bytes 6148
  109.7 18.3 %all-to-all-start.2 = ((f32[8,1,32768]{2,1,0:T(1,128)}), f32[8,1,32768]{2,1,0:T(1,128)}, u32[]{:S(2)}, u32[]{:S(2)}) async-start(f32[8,1,32768]{2,1,0:T(1,128)} %reshape.758), calls=%async_computation.2 | async-start | bytes 2097152 | tf_op jit(solution)/shard_map/all_to_all | solution.py:125
  116.1 58.0 %copy-start.43 = (f32[4,128]{1,0:T(4,128)}, f32[4,128]{1,0:T(4,128)S(1)}, u32[]{:S(2)}) copy-start(f32[4,128]{1,0:T(4,128)S(1)} %get-tuple-element.65) | copy-start | bytes 6148
  128.0 31.6 %all-to-all-start.3 = ((f32[8,1,32768]{2,1,0:T(1,128)}), f32[8,1,32768]{2,1,0:T(1,128)}, u32[]{:S(2)}, u32[]{:S(2)}) async-start(f32[8,1,32768]{2,1,0:T(1,128)} %reshape.760), calls=%async_computation.3 | async-start | bytes 2097152 | tf_op jit(solution)/shard_map/all_to_all | solution.py:126
  141.2 41.2 %copy-start.3 = (f32[1,16,32,4,128]{4,2,1,3,0:T(8,128)}, f32[1,16,32,4,128]{4,2,1,3,0:T(8,128)S(1)}, u32[]{:S(2)}) copy-start(f32[1,16,32,4,128]{4,2,1,3,0:T(8,128)S(1)} %get-tuple-element.35) | copy-start | bytes 3145732
  170.0 2.3 copy-start.18
  172.2 1.9 copy-start.22
  182.1 1.5 copy-start.15
  182.1 1.8 copy-start.16
  193.9 4.3 copy-start.1
  218.9 31.2 %all-to-all-start.5 = ((f32[8,1,65536]{2,1,0:T(1,128)}), f32[8,1,65536]{2,1,0:T(1,128)}, u32[]{:S(2)}, u32[]{:S(2)}) async-start(f32[8,1,65536]{2,1,0:T(1,128)} %reshape.764), calls=%async_computation.5 | async-start | bytes 4194304 | tf_op jit(solution)/shard_map/all_to_all | solution.py:135
  250.1 29.1 %all-to-all-start.4 = ((f32[8,1,65536]{2,1,0:T(1,128)}), f32[8,1,65536]{2,1,0:T(1,128)}, u32[]{:S(2)}, u32[]{:S(2)}) async-start(f32[8,1,65536]{2,1,0:T(1,128)} %reshape.762), calls=%async_computation.4 | async-start | bytes 4194304 | tf_op jit(solution)/shard_map/all_to_all | solution.py:134
  326.1 50.6 %all-to-all-start.6 = ((f32[4,1,131072]{2,1,0:T(1,128)}), f32[4,1,131072]{2,1,0:T(1,128)}, u32[]{:S(2)}, u32[]{:S(2)}) async-start(f32[4,1,131072]{2,1,0:T(1,128)} %reshape.766), calls=%async_computation.6 | async-start | bytes 4194304 | tf_op jit(solution)/shard_map/all_to_all | solution.py:143
  376.7 53.1 %all-to-all-start.7 = ((f32[4,1,131072]{2,1,0:T(1,128)}), f32[4,1,131072]{2,1,0:T(1,128)}, u32[]{:S(2)}, u32[]{:S(2)}) async-start(f32[4,1,131072]{2,1,0:T(1,128)} %reshape.768), calls=%async_computation.7 | async-start | bytes 4194304 | tf_op jit(solution)/shard_map/all_to_all | solution.py:144
  447.4 3.5 copy-start.17
  450.9 2.7 copy-start.10
  460.8 1.9 copy-start.26
  462.1 1.7 copy-start.24
  462.1 2.0 copy-start.25
  465.3 25.5 %copy-start.2 = (f32[3,64,32,128]{3,2,1,0:T(8,128)}, f32[3,64,32,128]{3,2,1,0:T(8,128)S(1)}, u32[]{:S(2)}) copy-start(f32[3,64,32,128]{3,2,1,0:T(8,128)S(1)} %fusion) | copy-start | bytes 9437188
  465.5 2.1 copy-start.5
  465.5 2.1 copy-start.7
  482.3 52.4 %all-to-all-start.9 = ((f32[4,1,131072]{2,1,0:T(1,128)}), f32[4,1,131072]{2,1,0:T(1,128)}, u32[]{:S(2)}, u32[]{:S(2)}) async-start(f32[4,1,131072]{2,1,0:T(1,128)} %reshape.772), calls=%async_computation.9 | async-start | bytes 4194304 | tf_op jit(solution)/shard_map/all_to_all | solution.py:117
  490.9 2.1 copy-start.6
  490.9 2.1 copy-start.8
  534.7 52.3 %all-to-all-start.8 = ((f32[4,1,131072]{2,1,0:T(1,128)}), f32[4,1,131072]{2,1,0:T(1,128)}, u32[]{:S(2)}, u32[]{:S(2)}) async-start(f32[4,1,131072]{2,1,0:T(1,128)} %reshape.770), calls=%async_computation.8 | async-start | bytes 4194304 | tf_op jit(solution)/shard_map/all_to_all | solution.py:116
  633.1 29.6 %all-to-all-start.10 = ((f32[8,1,65536]{2,1,0:T(1,128)}), f32[8,1,65536]{2,1,0:T(1,128)}, u32[]{:S(2)}, u32[]{:S(2)}) async-start(f32[8,1,65536]{2,1,0:T(1,128)} %reshape.774), calls=%async_computation.10 | async-start | bytes 4194304 | tf_op jit(solution)/shard_map/all_to_all | solution.py:125
  662.7 40.3 %all-to-all-start.11 = ((f32[8,1,65536]{2,1,0:T(1,128)}), f32[8,1,65536]{2,1,0:T(1,128)}, u32[]{:S(2)}, u32[]{:S(2)}) async-start(f32[8,1,65536]{2,1,0:T(1,128)} %reshape.776), calls=%async_computation.11 | async-start | bytes 4194304 | tf_op jit(solution)/shard_map/all_to_all | solution.py:126
  725.5 5.7 copy-start.9
  725.5 5.7 copy-start.44
  740.1 2.1 copy-start.4
  740.1 2.1 copy-start.11
  740.1 2.1 copy-start.12
  740.1 2.1 copy-start.13
  747.2 1.5 copy-start.47
  762.6 16.7 %all-to-all-start.13 = ((f32[8,1,32768]{2,1,0:T(1,128)}), f32[8,1,32768]{2,1,0:T(1,128)S(1)}, u32[]{:S(2)}, u32[]{:S(2)}) async-start(f32[8,1,32768]{2,1,0:T(1,128)} %reshape.780), calls=%async_computation.13 | async-start | bytes 2097152 | tf_op jit(solution)/shard_map/all_to_all | solution.py:135
  779.3 21.2 %all-to-all-start.12 = ((f32[8,1,32768]{2,1,0:T(1,128)}), f32[8,1,32768]{2,1,0:T(1,128)}, u32[]{:S(2)}, u32[]{:S(2)}) async-start(f32[8,1,32768]{2,1,0:T(1,128)} %reshape.778), calls=%async_computation.12 | async-start | bytes 2097152 | tf_op jit(solution)/shard_map/all_to_all | solution.py:134
  825.3 28.5 %all-to-all-start.15 = ((f32[4,1,65536]{2,1,0:T(1,128)}), f32[4,1,65536]{2,1,0:T(1,128)}, u32[]{:S(2)}, u32[]{:S(2)}) async-start(f32[4,1,65536]{2,1,0:T(1,128)} %reshape.784), calls=%async_computation.15 | async-start | bytes 2097152 | tf_op jit(solution)/shard_map/all_to_all | solution.py:144
  837.0 25.4 %copy-start.49 = (s32[4096]{0:T(1024)S(1)}, s32[4096]{0:T(1024)}, u32[]{:S(2)}) copy-start(s32[4096]{0:T(1024)} %param.12) | copy-start | bytes 49156
  853.8 29.9 %all-to-all-start.14 = ((f32[4,1,65536]{2,1,0:T(1,128)}), f32[4,1,65536]{2,1,0:T(1,128)}, u32[]{:S(2)}, u32[]{:S(2)}) async-start(f32[4,1,65536]{2,1,0:T(1,128)} %reshape.782), calls=%async_computation.14 | async-start | bytes 2097152 | tf_op jit(solution)/shard_map/all_to_all | solution.py:143
  890.9 4.0 copy-start.20
  890.9 4.0 copy-start.21
  890.9 4.0 copy-start.28
  895.0 7.1 copy-start.48
  (18 other events, 21.6 us)
where the time goes:
time: 943 us; the launch traced here: 926 us
  local copies, waits for them, and re-layouts  342 us (36%)
  matrix products  164 us (17%)
  waiting for transfers between devices  155 us (16%)
  other arithmetic  140 us (15%)
  starting transfers between devices  112 us (12%)
  between operations  12.8 us (1%)
    dot_general x58, matrix products, contract(): jnp.einsum(formula, operand, matrix, precision=highest, preferred_element...  159 us
    unnamed x132, local copies, waits for them, and re-layouts  139 us
    all_to_all x2, waiting for transfers between devices, lateral_forward(): lax.all_to_all(spectra[0], 'gx', split_axis=3, concat_axis=2, tiled=True)  37.8 us
    all_to_all x2, waiting for transfers between devices, lateral_forward(): lax.all_to_all(spectra[1], 'gx', split_axis=3, concat_axis=2, tiled=True)  37.5 us
    all_to_all x2, waiting for transfers between devices, lateral_inverse(): lax.all_to_all(spectra[1], 'gx', split_axis=2, concat_axis=3, tiled=True)  36 us
    all_to_all x2, waiting for transfers between devices, lateral_inverse(): lax.all_to_all(spectra[0], 'gx', split_axis=2, concat_axis=3, tiled=True)  35.3 us
    another operation x12, local copies, waits for them, and re-layouts  26 us
    scatter-add x1, other arithmetic, add_sources(): density.reshape(-1).at[flat_index].add(amounts, mode='drop')  22.8 us
  transfers between devices with their start and end apart: 16, of which 10 were waited for; matrix products, arithmetic and copies ran while one was open for 29% of the time, Pallas kernels for 0%

commit v1 on v0

v1 whole, which is shorter than its diff:
```python
import functools
import math

import numpy as np

import jax
import jax.numpy as jnp
from jax import lax
from jax.experimental import pallas as pl
from jax.experimental.pallas import tpu as pltpu
from jax.sharding import PartitionSpec as P

NZ = 512
NX = 128
NY = 128
LABELS = 8
PML_W = 20


time_step = 0.3
absorb = 2.0
high = lax.Precision.HIGHEST


def damping(positions, length, speed_ref):
    coordinate = positions.astype(jnp.float32)
    layer_depth = (
        jnp.maximum(jnp.maximum(PML_W - coordinate, coordinate - (length - 1 - PML_W)), 0.0) / PML_W
    )
    return jnp.exp(-absorb * speed_ref * layer_depth**4 * time_step * 0.5)


def add_sources(density, source_index, amounts, z_start, x_start):
    z_local, x_local, y_count = density.shape
    plane_size = NX * NY
    z_offset = source_index // plane_size - z_start
    remain = source_index % plane_size
    x_offset = remain // NY - x_start
    y_offset = remain % NY
    inside = (z_offset >= 0) & (z_offset < z_local) & (x_offset >= 0) & (x_offset < x_local)
    flat_index = jnp.where(
        inside, (z_offset * x_local + x_offset) * y_count + y_offset, z_local * x_local * y_count
    )
    return density.reshape(-1).at[flat_index].add(amounts, mode="drop").reshape(density.shape)


def real_basis(length):
    cells = np.arange(length)
    columns = np.zeros((length, length))
    waves = np.zeros(length)
    half = length // 2
    for index in range(half):
        angle = 2 * np.pi * index / length
        if index == 0:
            columns[:, 0] = 1 / np.sqrt(length)
            columns[:, 1] = np.cos(np.pi * cells) / np.sqrt(length)
            waves[1] = np.pi
        else:
            columns[:, 2 * index] = np.cos(angle * cells) * np.sqrt(2 / length)
            columns[:, 2 * index + 1] = np.sin(angle * cells) * np.sqrt(2 / length)
            waves[2 * index : 2 * index + 2] = angle
    return columns, waves


def staggered(length, orient):
    index = np.arange(length)
    wave = 2 * np.pi / length * np.where(index < length // 2, index, index - length)
    kernel = np.fft.ifft(1j * wave * np.exp(0.5j * orient * wave)).real
    return kernel[(index[:, None] - index[None, :]) % length]


def line_tables(length):
    basis, waves = real_basis(length)
    plus = staggered(length, 1.0) @ basis
    minus = staggered(length, -1.0).T @ basis
    return tuple(np.asarray(t, np.float32) for t in (basis, plus, minus)) + (waves,)


def contract(formula, operand, matrix):
    return jnp.einsum(formula, operand, matrix, precision=high, preferred_element_type=jnp.float32)


def packed_table(table, pack, z_devices):
    z_local = table.shape[0] // z_devices
    blocks = table.reshape(z_devices, 1, z_local, 1, table.shape[1])
    lines = np.eye(pack, dtype=np.float32).reshape(1, pack, 1, pack, 1)
    return (blocks * lines).reshape(z_devices, pack * z_local, pack * table.shape[1])


def exchange_kernel(axis, size, count, *refs):
    sources, targets = refs[:count], refs[count : 2 * count]
    held = refs[2 * count : 3 * count]
    send_sem, recv_sem, in_sem, out_sem = refs[3 * count :]
    me = lax.axis_index(axis)
    barrier = pltpu.get_barrier_semaphore()
    for step in range(1, size):
        pl.semaphore_signal(
            barrier,
            inc=1,
            device_id={axis: lax.rem(me + step, size)},
            device_id_type=pl.DeviceIdType.MESH,
        )
    locals_in = [
        pltpu.make_async_copy(sources[f].at[me], held[f], in_sem.at[f]) for f in range(count)
    ]
    for copy in locals_in:
        copy.start()
    pl.semaphore_wait(barrier, size - 1)
    copies = []
    for f in range(count):
        for step in range(1, size):
            peer = lax.rem(me + step, size)
            copy = pltpu.make_async_remote_copy(
                src_ref=sources[f].at[peer],
                dst_ref=targets[f].at[me],
                send_sem=send_sem.at[f, step],
                recv_sem=recv_sem.at[f, step],
                device_id={axis: peer},
                device_id_type=pl.DeviceIdType.MESH,
            )
            copy.start()
            copies.append(copy)
    locals_out = []
    for f in range(count):
        locals_in[f].wait()
        copy = pltpu.make_async_copy(held[f], targets[f].at[me], out_sem.at[f])
        copy.start()
        locals_out.append(copy)
    for copy in locals_out + copies:
        copy.wait()


def exchange(axis, size, name, *fields):
    count = len(fields)
    anywhere = pl.BlockSpec(memory_space=pl.ANY)
    return pl.pallas_call(
        functools.partial(exchange_kernel, axis, size, count),
        out_shape=[jax.ShapeDtypeStruct(f.shape, f.dtype) for f in fields],
        in_specs=[anywhere] * count,
        out_specs=[anywhere] * count,
        scratch_shapes=[pltpu.VMEM(f.shape[1:], f.dtype) for f in fields]
        + [
            pltpu.SemaphoreType.DMA((count, size)),
            pltpu.SemaphoreType.DMA((count, size)),
            pltpu.SemaphoreType.DMA((count,)),
            pltpu.SemaphoreType.DMA((count,)),
        ],
        compiler_params=pltpu.CompilerParams(collective_id=name, has_side_effects=True),
        name=f"exchange_{axis}_{name}",
    )(*fields)


def shards(density, velocity, labels, sound_table, mass_table, source_index, source_values):
    z_local, x_local, y_count = density.shape
    z_devices, x_devices = lax.axis_size("gz"), lax.axis_size("gx")
    z_start = lax.axis_index("gz") * z_local
    x_start = lax.axis_index("gx") * x_local
    speed_sq = jnp.zeros(density.shape, jnp.float32)
    rho_zero = jnp.zeros(density.shape, jnp.float32)
    for tissue in range(LABELS):
        chosen = labels == tissue
        speed_sq = jnp.where(chosen, sound_table[tissue] ** 2, speed_sq)
        rho_zero = jnp.where(chosen, mass_table[tissue], rho_zero)
    speed_ref = jnp.max(sound_table)
    damp_z = damping(z_start + jnp.arange(z_local, dtype=jnp.int32), NZ, speed_ref)[:, None, None]
    damp_x = damping(x_start + jnp.arange(x_local, dtype=jnp.int32), NX, speed_ref)[None, :, None]
    damp_y = damping(jnp.arange(y_count, dtype=jnp.int32), NY, speed_ref)[None, None, :]
    damp_all = damp_z * damp_x * damp_y
    z_basis, z_plus, z_minus, z_waves = line_tables(NZ)
    x_basis, x_plus, x_minus, x_waves = line_tables(NX)
    y_basis, y_plus, y_minus, y_waves = line_tables(NY)
    kx_local, ky_local = NX // z_devices, NY // x_devices
    pack = 2 if 2 * z_local <= 128 else 1
    groups = ky_local // pack
    lanes = pack * z_local
    z_tables = [packed_table(t, pack, z_devices) for t in (z_basis, z_plus, z_minus)]
    x_tables = [t.reshape(x_devices, x_local, z_devices, kx_local) for t in (x_basis, x_plus, x_minus)]
    y_tables = [t.reshape(y_count, x_devices * groups, pack) for t in (y_basis, y_plus, y_minus)]
    wave_x = lax.dynamic_slice_in_dim(
        jnp.asarray(x_waves, jnp.float32), lax.axis_index("gz") * kx_local, kx_local
    )[None, :, None]
    wave_y = lax.dynamic_slice_in_dim(
        jnp.asarray(y_waves, jnp.float32), lax.axis_index("gx") * ky_local, ky_local
    ).reshape(groups, 1, pack)
    wave_y = jnp.repeat(wave_y, NZ, axis=2)
    wave_z = jnp.asarray(np.tile(z_waves, pack), jnp.float32)[None, None, :]
    correction = jnp.sinc(
        speed_ref * jnp.sqrt(wave_z**2 + wave_x**2 + wave_y**2) * time_step / (2.0 * math.pi)
    )

    def y_forward(field, table):
        out = contract("zxy,yqp->qxpz", field, y_tables[table])
        return out.reshape(x_devices, groups, x_local, lanes)

    def x_forward(blocks, table):
        return contract("iqxl,ixdm->dqml", blocks, x_tables[table])

    def z_forward(blocks, table):
        return contract("dqml,dlc->qmc", blocks, z_tables[table])

    def z_inverse(spectrum, table):
        return contract("qmc,dlc->dqml", spectrum, z_tables[table])

    def x_inverse(blocks, table):
        return contract("dqml,ixdm->iqxl", blocks, x_tables[table])

    def y_inverse(blocks, table):
        blocks = blocks.reshape(x_devices * groups, x_local, pack, z_local)
        return contract("qxpz,yqp->zxy", blocks, y_tables[table])

    pressure = speed_sq * density
    (part,) = exchange("gx", x_devices, 0, y_forward(pressure, 0))
    (part,) = exchange("gz", z_devices, 1, x_forward(part, 0))
    spectrum = z_forward(part, 0) * correction
    along, plain = exchange("gz", z_devices, 2, z_inverse(spectrum, 1), z_inverse(spectrum, 0))
    along, across, plain = exchange(
        "gx", x_devices, 3, x_inverse(along, 0), x_inverse(plain, 1), x_inverse(plain, 0)
    )
    slope_z = y_inverse(along, 0)
    slope_x = y_inverse(across, 0)
    slope_y = y_inverse(plain, 1)
    ratio = time_step / rho_zero
    new_z = damp_z * (damp_z * velocity[0] - ratio * slope_z)
    new_x = damp_x * (damp_x * velocity[1] - ratio * slope_x)
    new_y = damp_y * (damp_y * velocity[2] - ratio * slope_y)
    along, across, plain = exchange(
        "gx", x_devices, 4, y_forward(new_z, 0), y_forward(new_x, 0), y_forward(new_y, 2)
    )
    along, plain = exchange(
        "gz", z_devices, 5, x_forward(along, 0), x_forward(across, 2) + x_forward(plain, 0)
    )
    spectrum = (z_forward(along, 2) + z_forward(plain, 0)) * correction
    (part,) = exchange("gz", z_devices, 6, z_inverse(spectrum, 0))
    (part,) = exchange("gx", x_devices, 7, x_inverse(part, 0))
    spread = y_inverse(part, 0)
    density = damp_all * (damp_all * density - time_step * rho_zero * spread)
    density = add_sources(density, source_index, source_values[0], z_start, x_start)
    return (density, jnp.stack([new_z, new_x, new_y]))


def solution(mesh):
    in_specs = (
        P("gz", "gx", None),
        P(None, "gz", "gx", None),
        P("gz", "gx", None),
        P(),
        P(),
        P(),
        P(),
    )
    out_specs = (P("gz", "gx", None), P(None, "gz", "gx", None))
    return jax.shard_map(shards, mesh=mesh, in_specs=in_specs, out_specs=out_specs, check_vma=False)
```

time: 943 us -> 485 us (0.51); the launches traced: 926 us -> 478 us
  local copies, waits for them, and re-layouts: 342 us -> 48.3 us
  Pallas kernels: 0 us -> 279 us
  waiting for transfers between devices: 155 us -> 0 us
  starting transfers between devices: 112 us -> 0 us
  other arithmetic: 140 us -> 28.2 us
  matrix products: 164 us -> 110 us
    pallas_call x0 -> x8, Pallas kernels: none -> 279 us  [exchange(): pl.pallas_call(functools.partial(exchange_kernel, axis, size, count), out...]
    all_to_all x16 -> x0, waiting for transfers between devices: 155 us -> none  [the longest x2 37.8 us: lateral_forward(): lax.all_to_all(spectra[0], 'gx', split_axis=3, concat_axis=2, tiled=True)]
    unnamed x132 -> x90, local copies, waits for them, and re-layouts: 139 us -> 6.61 us
    all_to_all x16 -> x0, starting transfers between devices: 112 us -> none  [the longest x2 16.7 us: lateral_forward(): lax.all_to_all(spectra[1], 'gx', split_axis=3, concat_axis=2, tiled=True)]
    all_to_all x16 -> x0, other arithmetic: 98.6 us -> none  [the longest x2 13.6 us: lateral_forward(): lax.all_to_all(spectra[0], 'gx', split_axis=3, concat_axis=2, tiled=True)]
    all_to_all x25 -> x0, local copies, waits for them, and re-layouts: 94 us -> none  [the longest x4 17.4 us: long_inverse(): lax.all_to_all(spectra[0], 'gz', split_axis=1, concat_axis=2, tiled=True)]
    dot_general x58 -> x22, matrix products: 159 us -> 110 us  [contract(): jnp.einsum(formula, operand, matrix, precision=high, preferred_element_ty...]
    another operation x15 -> x0, local copies, waits for them, and re-layouts: 26.5 us -> none
  transfers between devices with their start and end apart: 16 -> 0, of which waited for: 10 -> 0; matrix products, arithmetic and copies ran while one was open for 29% -> 0% of each run, Pallas kernels for 0% -> 0%
where the time goes in v1:
time: 485 us; the launch traced here: 478 us
  Pallas kernels  279 us (58%)
  matrix products  110 us (23%)
  local copies, waits for them, and re-layouts  48.3 us (10%)
  other arithmetic  28.2 us (6%)
  between operations  12.2 us (3%)
    pallas_call x8, Pallas kernels, exchange(): pl.pallas_call(functools.partial(exchange_kernel, axis, size, count), out...  279 us
    dot_general x22, matrix products, contract(): jnp.einsum(formula, operand, matrix, precision=high, preferred_element_ty...  110 us
    scatter-add x1, other arithmetic, add_sources(): density.reshape(-1).at[flat_index].add(amounts, mode='drop')  22.8 us
    reshape x4, local copies, waits for them, and re-layouts, y_forward(): return out.reshape(x_devices, groups, x_local, lanes)  13.7 us
    reshape x4, local copies, waits for them, and re-layouts, y_inverse(): blocks = blocks.reshape(x_devices * groups, x_local, pack, z_local)  12 us
    transpose x4, local copies, waits for them, and re-layouts, contract(): jnp.einsum(formula, operand, matrix, precision=high, preferred_element_ty...  11.3 us

profile of v1, /device:TPU:9, one launch (start us, length us, event | category | flops | bytes accessed | tf_op | source)
XLA Modules:
  0.0 477.6 jit_solution(2991690405623268414)
XLA Ops:
  0.6 1.6 fusion.105
  12.1 4.2 multiply_bitcast_fusion
  16.3 2.1 convolution_bitcast_fusion.3
  18.4 2.8 copy.91
  21.2 3.4 reshape.138.refs_0_
  24.6 26.5 %exchange_gx_0.1 = f32[4,16,32,128]{3,2,1,0:T(8,128)} custom-call(f32[4,16,32,128]{3,2,1,0:T(8,128)} %reshape.138.refs_0_), custom_call_target="tpu_custom_call" | custom-call | tf_op jit(solution)/shard_map/exchange_gx_0/pallas_call | solution.py:136
  51.2 3.3 convolution_bitcast_fusion.4.refs_0_
  54.5 15.5 %exchange_gz_1.1 = f32[8,16,16,128]{3,2,1,0:T(8,128)} custom-call(f32[8,16,16,128]{3,2,1,0:T(8,128)} %convolution_bitcast_fusion.4.refs_0_), custom_call_target="tpu_custom_call" | custom-call | tf_op jit(solution)/shard_map/exchange_gz_1/pallas_call | solution.py:136
  71.1 8.3 %fusion.21 = f32[16,16,1024,1]{2,1,0,3:T(8,128)S(1)} fusion(f32[8,16,16,128]{3,2,1,0:T(8,128)} %exchange_gz_1.1, f32[8,128,1024,1]{2,1,3,0:T(8,128)} %constant.201, f32[16,1024]{1,0:T(8,128)S(1)} %bitcast.256, f32[16,1024]{1,0:T(8,128)S(1)} %broadcast_add_fusion, f32[]{:T(128)} %reduce_max.9), kind=kOutput, calls=%fused_computation.41 | convolution fusion | flops 3230924800 | bytes 6422532 | tf_op jit(solution)/shard_map/dqml,dlc->qmc/dot_general | solution.py:80
  79.4 4.7 convolution_bitcast_fusion.15.refs_1_
  84.1 4.7 convolution_bitcast_fusion.16.refs_0_
  88.8 26.5 %exchange_gz_2.1 = (f32[8,16,16,128]{3,2,1,0:T(8,128)}, f32[8,16,16,128]{3,2,1,0:T(8,128)}) custom-call(f32[8,16,16,128]{3,2,1,0:T(8,128)} %convolution_bitcast_fusion.16.refs_0_, f32[8,16,16,128]{3,2,1,0:T(8,128)} %convolution_bitcast_fusion.15.refs_1_), custom_call_target="tpu_custom_call" | custom-call | tf_op jit(solution)/shard_map/exchange_gz_2/pallas_call | solution.py:136
  115.3 3.4 convolution_bitcast_fusion.12.refs_2_
  118.8 2.1 convolution_bitcast_fusion.13.refs_1_
  120.9 2.1 convolution_bitcast_fusion.14.refs_0_
  122.9 71.7 %exchange_gx_3.1 = (f32[4,16,32,128]{3,2,1,0:T(8,128)}, f32[4,16,32,128]{3,2,1,0:T(8,128)}, f32[4,16,32,128]{3,2,1,0:T(8,128)}) custom-call(f32[4,16,32,128]{3,2,1,0:T(8,128)} %convolution_bitcast_fusion.14.refs_0_, f32[4,16,32,128]{3,2,1,0:T(8,128)} %convolution_bitcast_fusion.13.refs_1_, f32[4,16,32,128]{3,2,1,0:T(8,128)} %convolution_bitcast_fusion.12.refs_2_), custom_call_target="tpu_custom_call" | custom-call | tf_op jit(solution)/shard_map/exchange_gx_3/pallas_call | solution.py:136
  194.7 3.7 reshape.143
  199.8 1.6 fusion.103
  202.6 9.8 %fusion.39 = f32[64,32,128]{2,0,1:T(8,128)S(1)} fusion(f32[128,64,2,1]{0,1,2,3:T(8,128)S(1)} %copy-done.42, f32[64,32,2,64]{3,2,1,0:T(2,128)S(1)} %copy-done.11, f32[1,64,32,128]{3,2,1,0:T(8,128)S(1)} %get-tuple-element.35, f32[128]{0:T(128)S(1)} %multiply_exponential_fusion, pred[64,32,128]{2,0,1:T(32,128)(4,1)S(1)} %copy-done.29, ...), kind=kOutput, calls=%fused_computation.49 | convolution fusion | flops 406061056 | bytes 5308960 | tf_op jit(solution)/shard_map/qxpz,yqp->zxy/dot_general | solution.py:80
  212.5 2.5 reshape.141
  215.0 12.7 %fusion.48 = f32[64,32,128]{2,0,1:T(8,128)S(1)} fusion(f32[128,64,2,1]{0,1,2,3:T(8,128)S(1)} %copy-done.18, f32[64,32,2,64]{3,2,1,0:T(2,128)} %reshape.141, f32[1,64,32,128]{3,2,1,0:T(8,128)} %get-tuple-element.36, f32[32]{0:T(128)S(1)} %multiply_exponential_fusion.1, pred[64,32,128]{2,0,1:T(32,128)(4,1)} %get-tuple-element.34, ...), kind=kOutput, calls=%fused_computation.52 | convolution fusion | flops 406061056 | bytes 5308576 | tf_op jit(solution)/shard_map/qxpz,yqp->zxy/dot_general | solution.py:80
  227.7 2.9 reshape.139
  230.6 12.3 %fusion.57 = f32[64,32,128]{2,0,1:T(8,128)S(1)} fusion(f32[128,64,2,1]{0,1,2,3:T(8,128)S(1)} %copy-done.18, f32[64,32,2,64]{3,2,1,0:T(2,128)} %reshape.139, f32[1,64,32,128]{3,2,1,0:T(8,128)} %get-tuple-element.37, f32[64]{0:T(128)S(1)} %multiply_exponential_fusion.2, pred[64,32,128]{2,0,1:T(32,128)(4,1)} %get-tuple-element.34, ...), kind=kOutput, calls=%fused_computation.55 | convolution fusion | flops 406061056 | bytes 5308704 | tf_op jit(solution)/shard_map/qxpz,yqp->zxy/dot_general | solution.py:80
  243.9 3.5 copy.124
  247.4 2.1 convolution_bitcast_fusion
  249.6 2.9 copy.111
  252.4 3.6 reshape.144.refs_2_
  256.0 2.1 convolution_bitcast_fusion.1
  258.2 2.9 copy.107
  261.0 3.4 reshape.142.refs_1_
  264.4 2.1 convolution_bitcast_fusion.2
  266.6 2.9 copy.103
  269.5 3.3 reshape.140.refs_0_
  272.8 71.5 %exchange_gx_4.1 = (f32[4,16,32,128]{3,2,1,0:T(8,128)}, f32[4,16,32,128]{3,2,1,0:T(8,128)}, f32[4,16,32,128]{3,2,1,0:T(8,128)}) custom-call(f32[4,16,32,128]{3,2,1,0:T(8,128)} %reshape.140.refs_0_, f32[4,16,32,128]{3,2,1,0:T(8,128)} %reshape.142.refs_1_, f32[4,16,32,128]{3,2,1,0:T(8,128)} %reshape.144.refs_2_), custom_call_target="tpu_custom_call" | custom-call | tf_op jit(solution)/shard_map/exchange_gx_4/pallas_call | solution.py:136
  344.3 2.4 convolution_bitcast_fusion.9
  346.7 2.1 fusion.61.refs_1_
  348.8 2.1 convolution_bitcast_fusion.11.refs_0_
  350.9 26.0 %exchange_gz_5.1 = (f32[8,16,16,128]{3,2,1,0:T(8,128)}, f32[8,16,16,128]{3,2,1,0:T(8,128)}) custom-call(f32[8,16,16,128]{3,2,1,0:T(8,128)} %convolution_bitcast_fusion.11.refs_0_, f32[8,16,16,128]{3,2,1,0:T(8,128)} %fusion.61.refs_1_), custom_call_target="tpu_custom_call" | custom-call | tf_op jit(solution)/shard_map/exchange_gz_5/pallas_call | solution.py:136
  377.0 6.4 %convolution_bitcast_fusion.7 = f32[16,16,1024]{2,1,0:T(8,128)S(1)} fusion(f32[8,16,16,128]{3,2,1,0:T(8,128)} %get-tuple-element.21, f32[8,128,1024,1]{2,1,3,0:T(8,128)} %constant.201), kind=kOutput, calls=%fused_computation.29 | convolution fusion | flops 3221225472 | bytes 6291456 | tf_op jit(solution)/shard_map/dqml,dlc->qmc/dot_general | solution.py:80
  383.4 5.7 %fusion.24 = f32[16,16,1024,1]{2,1,0,3:T(8,128)S(1)} fusion(f32[16,16,1024]{2,1,0:T(8,128)S(1)} %convolution_bitcast_fusion.7, f32[8,16,16,128]{3,2,1,0:T(8,128)S(1)} %copy-done.40, f32[8,128,1024,1]{2,1,3,0:T(8,128)S(1)} %copy-done.41, f32[16,1024]{1,0:T(8,128)S(1)} %bitcast.257, f32[16,1024]{1,0:T(8,128)S(1)} %copy-done.33, f32[]{:T(128)} %reduce_max.9), kind=kOutput, calls=%fused_computation.44 | convolution fusion | flops 3231186944 | bytes 7471108 | tf_op jit(solution)/shard_map/dqml,dlc->qmc/dot_general | solution.py:80
  389.1 4.7 convolution_bitcast_fusion.6.refs_0_
  393.8 15.1 %exchange_gz_6.1 = f32[8,16,16,128]{3,2,1,0:T(8,128)} custom-call(f32[8,16,16,128]{3,2,1,0:T(8,128)} %convolution_bitcast_fusion.6.refs_0_), custom_call_target="tpu_custom_call" | custom-call | tf_op jit(solution)/shard_map/exchange_gz_6/pallas_call | solution.py:136
  408.9 3.3 convolution_bitcast_fusion.5.refs_0_
  412.2 25.9 %exchange_gx_7.1 = f32[4,16,32,128]{3,2,1,0:T(8,128)} custom-call(f32[4,16,32,128]{3,2,1,0:T(8,128)} %convolution_bitcast_fusion.5.refs_0_), custom_call_target="tpu_custom_call" | custom-call | tf_op jit(solution)/shard_map/exchange_gx_7/pallas_call | solution.py:136
  438.1 2.8 reshape.145
  441.1 11.5 %multiply_multiply_fusion = f32[64,32,128]{2,0,1:T(8,128)S(1)} fusion(f32[128,64,2,1]{0,1,2,3:T(8,128)S(1)} %copy-done.18, f32[64,32,2,64]{3,2,1,0:T(2,128)S(1)} %reshape.145, f32[64,32,128]{2,1,0:T(8,128)S(1)} %copy-done.15, f32[128]{0:T(128)S(1)} %multiply_exponential_fusion, f32[64,32]{0,1:T(8,128)S(1)} %broadcast_multiply_fusion, ...), kind=kOutput, calls=%fused_computation.16 | convolution fusion | flops 406323200 | bytes 5317152 | tf_op jit(solution)/shard_map/qxpz,yqp->zxy/dot_general | solution.py:80
  453.4 22.8 %scatter_fusion = f32[262144]{0:T(1024)S(1)} fusion(f32[262144]{0:T(1024)S(1)} %bitcast.247, s32[4096]{0:T(1024)S(1)} %compare_select_fusion, f32[4096]{0:T(1024)S(1)} %bitcast.258), kind=kCustom, calls=%fused_computation | custom fusion | flops 4096 | bytes 65536 | tf_op jit(solution)/shard_map/scatter-add | solution.py:44
  476.2 1.0 copy-done
  (102 shorter events, 4.9 us)
Async XLA Ops:
  12.1 4.2 copy-start.18
  21.2 29.9 %copy-start.19 = (f32[4,32,8,16,1]{1,3,0,4,2:T(8,128)S(1)}, f32[4,32,8,16,1]{1,3,0,4,2:T(8,128)}, u32[]{:S(2)}) copy-start(f32[4,32,8,16,1]{1,3,0,4,2:T(8,128)} %constant.200) | copy-start | bytes 196612
  51.1 18.9 %copy-start.43 = (f32[128]{0:T(128)S(1)}, f32[128]{0:T(128)}, u32[]{:S(2)}) copy-start(f32[128]{0:T(128)} %constant.186.clone) | copy-start | bytes 1540
  51.1 19.3 %copy-start.38 = (f32[1024]{0:T(1024)S(1)}, f32[1024]{0:T(1024)}, u32[]{:S(2)}) copy-start(f32[1024]{0:T(1024)} %constant.197) | copy-start | bytes 12292
  51.1 19.3 %copy-start.34 = (f32[8]{0:T(128)S(1)}, f32[8]{0:T(128)}, u32[]{:S(2)}) copy-start(f32[8]{0:T(128)} %param.35) | copy-start | bytes 100
  70.5 8.9 %copy-start.32 = (f32[16,1024]{1,0:T(8,128)}, f32[16,1024]{1,0:T(8,128)S(1)}, u32[]{:S(2)}) copy-start(f32[16,1024]{1,0:T(8,128)S(1)} %broadcast_add_fusion) | copy-start | bytes 196612
  71.1 8.3 %copy-start.1 = (f32[8,128,1024,1]{2,1,3,0:T(8,128)S(1)}, f32[8,128,1024,1]{2,1,3,0:T(8,128)}, u32[]{:S(2)}) copy-start(f32[8,128,1024,1]{2,1,3,0:T(8,128)} %constant.201) | copy-start | bytes 12582916
  79.4 4.7 copy-start.3
  88.8 26.5 %copy-start.10 = (f32[4,32,8,16,1]{1,3,2,4,0:T(8,128)S(1)}, f32[4,32,8,16,1]{1,3,2,4,0:T(8,128)}, u32[]{:S(2)}) copy-start(f32[4,32,8,16,1]{1,3,2,4,0:T(8,128)} %constant.203) | copy-start | bytes 196612
  88.8 29.9 %copy-start.30 = (f32[4,32,8,16,1]{1,3,2,4,0:T(8,128)S(1)}, f32[4,32,8,16,1]{1,3,2,4,0:T(8,128)}, u32[]{:S(2)}) copy-start(f32[4,32,8,16,1]{1,3,2,4,0:T(8,128)} %constant.204) | copy-start | bytes 196612
  115.3 3.5 copy-start.8
  115.3 5.5 %copy-start.14 = (f32[8,16,16,128]{3,2,1,0:T(8,128)S(1)}, f32[8,16,16,128]{3,2,1,0:T(8,128)}, u32[]{:S(2)}) copy-start(f32[8,16,16,128]{3,2,1,0:T(8,128)} %get-tuple-element.12) | copy-start | bytes 3145732
  194.6 3.7 copy-start.35
  194.6 5.0 %copy-start.9 = (f32[3,64,32,128]{3,2,1,0:T(8,128)S(1)}, f32[3,64,32,128]{3,2,1,0:T(8,128)}, u32[]{:S(2)}) copy-start(f32[3,64,32,128]{3,2,1,0:T(8,128)} %param.33) | copy-start | bytes 9437188
  199.7 2.1 copy-start.11
  199.7 2.3 copy-start.21
  199.7 2.4 copy-start.23
  199.7 2.5 copy-start.24
  199.7 2.5 copy-start.25
  199.8 2.6 copy-start.26
  199.8 2.7 copy-start.27
  199.8 2.7 copy-start.28
  199.8 2.8 copy-start.29
  199.8 2.8 copy-start.42
  202.6 9.9 %copy-start.13 = (f32[4,16,32,128]{3,2,1,0:T(8,128)S(1)}, f32[4,16,32,128]{3,2,1,0:T(8,128)}, u32[]{:S(2)}) copy-start(f32[4,16,32,128]{3,2,1,0:T(8,128)} %get-tuple-element.15) | copy-start | bytes 3145732
  215.0 12.7 %copy-start.12 = (f32[4,16,32,128]{3,2,1,0:T(8,128)S(1)}, f32[4,16,32,128]{3,2,1,0:T(8,128)}, u32[]{:S(2)}) copy-start(f32[4,16,32,128]{3,2,1,0:T(8,128)} %get-tuple-element.14) | copy-start | bytes 3145732
  227.6 15.3 %copy-start.4 = (f32[64,32,128]{2,0,1:T(8,128)}, f32[64,32,128]{2,0,1:T(8,128)S(1)}, u32[]{:S(2)}) copy-start(f32[64,32,128]{2,0,1:T(8,128)S(1)} %fusion.48) | copy-start | bytes 3145732
  242.9 1.0 copy-start.6
  243.9 3.5 copy-start.31
  252.4 3.6 copy-start.5
  261.0 3.4 copy-start.7
  272.8 71.5 %copy-start.20 = (f32[4,32,8,16,1]{1,3,0,4,2:T(8,128)S(1)}, f32[4,32,8,16,1]{1,3,0,4,2:T(8,128)}, u32[]{:S(2)}) copy-start(f32[4,32,8,16,1]{1,3,0,4,2:T(8,128)} %constant.200) | copy-start | bytes 196612
  272.8 73.9 %copy-start.17 = (f32[4,32,8,16,1]{1,3,0,4,2:T(8,128)S(1)}, f32[4,32,8,16,1]{1,3,0,4,2:T(8,128)}, u32[]{:S(2)}) copy-start(f32[4,32,8,16,1]{1,3,0,4,2:T(8,128)} %constant.207) | copy-start | bytes 196612
  344.3 2.4 copy-start.16
  346.7 2.1 copy-start.39
  376.9 6.4 %copy-start.33 = (f32[16,1024]{1,0:T(8,128)S(1)}, f32[16,1024]{1,0:T(8,128)}, u32[]{:S(2)}) copy-start(f32[16,1024]{1,0:T(8,128)} %copy-done.32) | copy-start | bytes 196612
  377.0 6.4 %copy-start.40 = (f32[8,16,16,128]{3,2,1,0:T(8,128)S(1)}, f32[8,16,16,128]{3,2,1,0:T(8,128)}, u32[]{:S(2)}) copy-start(f32[8,16,16,128]{3,2,1,0:T(8,128)} %get-tuple-element.20) | copy-start | bytes 3145732
  377.0 6.4 %copy-start.41 = (f32[8,128,1024,1]{2,1,3,0:T(8,128)S(1)}, f32[8,128,1024,1]{2,1,3,0:T(8,128)}, u32[]{:S(2)}) copy-start(f32[8,128,1024,1]{2,1,3,0:T(8,128)} %constant.208) | copy-start | bytes 12582916
  383.4 5.7 %copy-start.2 = (f32[8,128,1024,1]{2,1,3,0:T(8,128)S(1)}, f32[8,128,1024,1]{2,1,3,0:T(8,128)}, u32[]{:S(2)}) copy-start(f32[8,128,1024,1]{2,1,3,0:T(8,128)} %constant.201) | copy-start | bytes 12582916
  438.1 3.0 copy-start.15
  438.1 2.9 copy-start.22
  452.6 0.7 copy-start.37
  452.6 0.8 copy-start.36
  476.2 1.0 copy-start
